TPU v7x, 32 devices: a whole 2x2x4 slice. The times are simulated.
32 devices in a mesh: dp: 16 (over z, x, core), tensor: 2 (over y).
Axes of the slice: x: 2, y: 2, z: 4, core: 2. Of those that a mesh axis runs over, the one named last changes fastest.
Arguments:
- x_in: bfloat16 [16, 2, 1024, 768], P(None, 'tensor', 'dp'), may hold values from -6 to 6
- cotangent: bfloat16 [16, 2, 1024, 768], P(None, 'tensor', 'dp'), may hold values from -6 to 6
- lengths: int32 [16], replicated, may hold values from 1 to 2048, 24576 in all
- dealing: int32 [16], replicated, may hold values from 0 to 15, each once
- w_qkv: float32 [768, 3, 768], P('dp', None, 'tensor'), may hold values from -0.21875 to 0.21875
- w_out: float32 [768, 768], P('dp', 'tensor'), may hold values from -1.75 to 1.75
- w_in: float32 [768, 3072], P('dp', 'tensor'), may hold values from -0.21875 to 0.21875
- w_ffo: float32 [768, 3072], P('dp', 'tensor'), may hold values from -0.109375 to 0.109375
- b_qv: float32 [2, 768], P(None, 'tensor'), may hold values from -3 to 3
- b_out: float32 [768], replicated, may hold values from -3 to 3
- b_in: float32 [3072], P('tensor'), may hold values from -3 to 3
- b_ffo: float32 [768], replicated, may hold values from -3 to 3
- ln1_gain: float32 [768], replicated, may hold values from 0.1 to 1.9
- ln1_bias: float32 [768], replicated, may hold values from -3 to 3
- ln2_gain: float32 [768], replicated, may hold values from 0.1 to 1.9
- ln2_bias: float32 [768], replicated, may hold values from -3 to 3
Outputs:
- out: bfloat16 [16, 2, 1024, 768], P(None, 'tensor', 'dp')
- grad_in: bfloat16 [16, 2, 1024, 768], P(None, 'tensor', 'dp')
- grad_w_qkv: float32 [768, 3, 768], P('dp', None, 'tensor')
- grad_w_out: float32 [768, 768], P('dp', 'tensor')
- grad_w_in: float32 [768, 3072], P('dp', 'tensor')
- grad_w_ffo: float32 [768, 3072], P('dp', 'tensor')
- grad_b_qv: float32 [2, 768], P(None, 'tensor')
- grad_b_out: float32 [768], replicated
- grad_b_in: float32 [3072], P('tensor')
- grad_b_ffo: float32 [768], replicated
- grad_ln1_gain: float32 [768], replicated
- grad_ln1_bias: float32 [768], replicated
- grad_ln2_gain: float32 [768], replicated
- grad_ln2_bias: float32 [768], replicated
Inputs may be any that keep to these rules, and one draw needn't show every extreme that they name: Slot j holds lengths[j] tokens of its sequence and padding after them; some slot is full, 2048 tokens. Sequence s goes to slot dealing[s]; every slot gets one sequence.
All inputs are finite; a program needn't handle non-finite values.
Results may differ from a plain program's by a relative error of at most 0.018.
Values may be sent and summed in bfloat16 or wider, within the bound.
A program may use at most 192 MiB of HBM per device.

v0:
```python
import jax
import jax.numpy as jnp
from jax import lax
from jax.sharding import PartitionSpec as P

HEAD_DIM = 64


def slot_owner(dealing):
    places = jnp.arange(dealing.shape[0], dtype=jnp.int32)
    matches = dealing[None, :] == places[:, None]
    return jnp.sum(jnp.where(matches, places[None, :], 0), axis=1)


def contract_last(left_side, right_side):
    return lax.dot_general(
        left_side, right_side, (((1,), (1,)), ((), ())), preferred_element_type=jnp.float32
    )


def contract_first(left_side, right_side):
    return lax.dot_general(
        left_side, right_side, (((0,), (0,)), ((), ())), preferred_element_type=jnp.float32
    )


def norm_forward(values, norm_gain, norm_shift):
    centre = jnp.mean(values, axis=-1, keepdims=True)
    centred = values - centre
    inverse = lax.rsqrt(jnp.mean(centred * centred, axis=-1, keepdims=True) + 1e-06)
    normed = centred * inverse
    return (normed * norm_gain + norm_shift, normed, inverse)


def norm_backward(upstream, normed, inverse, norm_gain):
    scaled = upstream * norm_gain
    back_rows = inverse * (
        scaled
        - jnp.mean(scaled, axis=-1, keepdims=True)
        - normed * jnp.mean(scaled * normed, axis=-1, keepdims=True)
    )
    return (back_rows, jnp.sum(upstream * normed, axis=0), jnp.sum(upstream, axis=0))


def gelu_slope(values):
    return (
        0.5 * (1.0 + lax.erf(values * 0.7071067811865476))
        + values * jnp.exp(-0.5 * values * values) * 0.3989422804014327
    )


def head_forward(query_rows, key_rows, value_rows, key_valid, block_rows, score_scale):
    outputs = []
    totals = []
    for row_start in range(0, query_rows.shape[0], block_rows):
        scores = (
            contract_last(query_rows[row_start : row_start + block_rows], key_rows) * score_scale
        )
        scores = jnp.where(key_valid[None, :], scores, -jnp.inf)
        maxima = jnp.max(scores, axis=1, keepdims=True)
        weights = jnp.exp(scores - maxima)
        summed = jnp.sum(weights, axis=1, keepdims=True)
        probs_low = (weights / summed).astype(jnp.bfloat16)
        outputs.append(jnp.dot(probs_low, value_rows, preferred_element_type=jnp.float32))
        totals.append((maxima + jnp.log(summed))[:, 0])
    return (jnp.concatenate(outputs, axis=0), jnp.concatenate(totals, axis=0))


def head_backward(
    query_rows, key_rows, value_rows, mixed_grad, log_totals, key_valid, block_rows, score_scale
):
    key_grad = jnp.zeros(key_rows.shape, jnp.float32)
    value_grad = jnp.zeros(value_rows.shape, jnp.float32)
    query_parts = []
    for row_start in range(0, query_rows.shape[0], block_rows):
        query_block = query_rows[row_start : row_start + block_rows]
        grad_block = mixed_grad[row_start : row_start + block_rows]
        scores = contract_last(query_block, key_rows) * score_scale
        scores = jnp.where(key_valid[None, :], scores, -jnp.inf)
        probs = jnp.exp(scores - log_totals[row_start : row_start + block_rows][:, None])
        prob_grad = contract_last(grad_block, value_rows)
        shared = jnp.sum(probs * prob_grad, axis=1, keepdims=True)
        score_grad = (probs * (prob_grad - shared)).astype(jnp.bfloat16)
        query_parts.append(
            jnp.dot(score_grad, key_rows, preferred_element_type=jnp.float32) * score_scale
        )
        key_grad = key_grad + contract_first(score_grad, query_block) * score_scale
        value_grad = value_grad + contract_first(probs.astype(jnp.bfloat16), grad_block)
    return (jnp.concatenate(query_parts, axis=0), key_grad, value_grad)


def per_device(
    x_in,
    cotangent,
    lengths,
    dealing,
    w_qkv,
    w_out,
    w_in,
    w_ffo,
    b_qv,
    b_out,
    b_in,
    b_ffo,
    ln1_gain,
    ln1_bias,
    ln2_gain,
    ln2_bias,
):
    owners = slot_owner(dealing)
    dealt_x, dealt_grad = (
        lax.all_to_all(
            jnp.take(x_in, owners, axis=0), "dp", split_axis=0, concat_axis=2, tiled=True
        ),
        lax.all_to_all(
            jnp.take(cotangent, owners, axis=0), "dp", split_axis=0, concat_axis=2, tiled=True
        ),
    )
    tokens_half = dealt_x[0, 0]
    output_grad = dealt_grad[0, 0].astype(jnp.float32)
    half_rows = tokens_half.shape[0]
    tensor_count = lax.axis_size("tensor")
    tensor_index = lax.axis_index("tensor")
    seq_rows = half_rows * tensor_count
    model_width = tokens_half.shape[1]
    head_width = b_qv.shape[1]
    head_count = head_width // HEAD_DIM
    ffn_width = b_in.shape[0]
    block_rows = min(512, seq_rows)
    score_scale = HEAD_DIM ** (-0.5)
    key_valid = jnp.arange(seq_rows) < lengths[lax.axis_index("dp")]
    qkv_weight, out_weight, in_weight, ffo_weight = (
        lax.all_gather(w_qkv.astype(jnp.bfloat16), "dp", axis=0, tiled=True),
        lax.all_gather(w_out.astype(jnp.bfloat16), "dp", axis=0, tiled=True),
        lax.all_gather(w_in.astype(jnp.bfloat16), "dp", axis=0, tiled=True),
        lax.all_gather(w_ffo.astype(jnp.bfloat16), "dp", axis=0, tiled=True),
    )

    def split_heads(matrix):
        return matrix.reshape(seq_rows, head_count, HEAD_DIM).transpose(1, 0, 2)

    def merge_heads(stacked):
        return stacked.transpose(1, 0, 2).reshape(seq_rows, head_width)

    tokens_full = lax.all_gather(tokens_half, "tensor", axis=0, tiled=True)
    projected = jnp.einsum(
        "ld,dce->cle", tokens_full, qkv_weight, preferred_element_type=jnp.float32
    )
    query_heads = split_heads((projected[0] + b_qv[0]).astype(jnp.bfloat16))
    key_heads = split_heads(projected[1].astype(jnp.bfloat16))
    value_heads = split_heads((projected[2] + b_qv[1]).astype(jnp.bfloat16))
    mixed_heads, log_totals = lax.map(
        lambda triple: head_forward(
            triple[0], triple[1], triple[2], key_valid, block_rows, score_scale
        ),
        (query_heads, key_heads, value_heads),
    )
    mixed_low = merge_heads(mixed_heads).astype(jnp.bfloat16)
    attn_half = lax.psum_scatter(
        contract_last(
            lax.slice_in_dim(mixed_low, 0, lax.axis_size("tensor") * half_rows, axis=0), out_weight
        ).astype(jnp.bfloat16),
        "tensor",
        scatter_dimension=0,
        tiled=True,
    ).astype(jnp.float32)
    first_norm, normed_one, inverse_one = norm_forward(
        tokens_half.astype(jnp.float32) + attn_half + b_out, ln1_gain, ln1_bias
    )
    first_full = lax.all_gather(first_norm.astype(jnp.bfloat16), "tensor", axis=0, tiled=True)
    hidden = jnp.dot(first_full, in_weight, preferred_element_type=jnp.float32) + b_in
    active = jax.nn.gelu(hidden, approximate=False).astype(jnp.bfloat16)
    ffn_half = lax.psum_scatter(
        contract_last(
            lax.slice_in_dim(active, 0, lax.axis_size("tensor") * half_rows, axis=0), ffo_weight
        ).astype(jnp.bfloat16),
        "tensor",
        scatter_dimension=0,
        tiled=True,
    ).astype(jnp.float32)
    result, normed_two, inverse_two = norm_forward(
        first_norm + ffn_half + b_ffo, ln2_gain, ln2_bias
    )
    final_grad, gain_two_grad, shift_two_grad = norm_backward(
        output_grad, normed_two, inverse_two, ln2_gain
    )
    ffo_bias_grad = jnp.sum(final_grad, axis=0)
    qkv_weight, out_weight, in_weight, ffo_weight = (
        lax.all_gather(w_qkv.astype(jnp.bfloat16), "dp", axis=0, tiled=True),
        lax.all_gather(w_out.astype(jnp.bfloat16), "dp", axis=0, tiled=True),
        lax.all_gather(w_in.astype(jnp.bfloat16), "dp", axis=0, tiled=True),
        lax.all_gather(w_ffo.astype(jnp.bfloat16), "dp", axis=0, tiled=True),
    )
    ffn_grad_full = lax.all_gather(final_grad.astype(jnp.bfloat16), "tensor", axis=0, tiled=True)
    ffo_weight_grad = contract_first(ffn_grad_full, active)
    hidden_grad = (
        jnp.dot(ffn_grad_full, ffo_weight, preferred_element_type=jnp.float32) * gelu_slope(hidden)
    ).astype(jnp.bfloat16)
    in_weight_grad = contract_first(first_full, hidden_grad)
    in_bias_grad = jnp.sum(hidden_grad.astype(jnp.float32), axis=0)
    first_grad = final_grad + lax.psum_scatter(
        contract_last(
            lax.slice_in_dim(hidden_grad, 0, lax.axis_size("tensor") * half_rows, axis=0), in_weight
        ).astype(jnp.bfloat16),
        "tensor",
        scatter_dimension=0,
        tiled=True,
    ).astype(jnp.float32)
    resid_grad, gain_one_grad, shift_one_grad = norm_backward(
        first_grad, normed_one, inverse_one, ln1_gain
    )
    out_bias_grad = jnp.sum(resid_grad, axis=0)
    attn_grad_full = lax.all_gather(resid_grad.astype(jnp.bfloat16), "tensor", axis=0, tiled=True)
    out_weight_grad = contract_first(attn_grad_full, mixed_low)
    mixed_grad = jnp.dot(attn_grad_full, out_weight, preferred_element_type=jnp.float32).astype(
        jnp.bfloat16
    )
    query_grads, key_grads, value_grads = lax.map(
        lambda bundle: head_backward(
            bundle[0],
            bundle[1],
            bundle[2],
            bundle[3],
            bundle[4],
            key_valid,
            block_rows,
            score_scale,
        ),
        (query_heads, key_heads, value_heads, split_heads(mixed_grad), log_totals),
    )
    qkv_grad = jnp.stack(
        [merge_heads(query_grads), merge_heads(key_grads), merge_heads(value_grads)]
    ).astype(jnp.bfloat16)
    qv_bias_grad = jnp.stack(
        [
            jnp.sum(qkv_grad[0].astype(jnp.float32), axis=0),
            jnp.sum(qkv_grad[2].astype(jnp.float32), axis=0),
        ]
    )
    qkv_weight_grad = jnp.einsum(
        "ld,cle->dce", tokens_full, qkv_grad, preferred_element_type=jnp.float32
    )
    rows_grad = lax.slice_in_dim(qkv_grad, 0, lax.axis_size("tensor") * half_rows, axis=1)
    input_grad = resid_grad + lax.psum_scatter(
        jnp.einsum("cle,dce->ld", rows_grad, qkv_weight, preferred_element_type=jnp.float32).astype(
            jnp.bfloat16
        ),
        "tensor",
        scatter_dimension=0,
        tiled=True,
    ).astype(jnp.float32)
    qkv_sum, out_sum, in_sum, ffo_sum = (
        lax.psum_scatter(qkv_weight_grad, "dp", scatter_dimension=0, tiled=True),
        lax.psum_scatter(out_weight_grad, "dp", scatter_dimension=0, tiled=True),
        lax.psum_scatter(in_weight_grad, "dp", scatter_dimension=0, tiled=True),
        lax.psum_scatter(ffo_weight_grad, "dp", scatter_dimension=0, tiled=True),
    )
    norm_terms = jnp.stack(
        [out_bias_grad, ffo_bias_grad, gain_one_grad, shift_one_grad, gain_two_grad, shift_two_grad]
    )
    qv_padded = lax.dynamic_update_slice_in_dim(
        jnp.zeros((2, model_width), jnp.float32), qv_bias_grad, tensor_index * head_width, 1
    )
    in_padded = lax.dynamic_update_slice_in_dim(
        jnp.zeros((ffn_width * tensor_count,), jnp.float32),
        in_bias_grad,
        tensor_index * ffn_width,
        0,
    )
    norm_sums, qv_sums, in_sums = lax.psum((norm_terms, qv_padded, in_padded), ("dp", "tensor"))
    qv_share = lax.dynamic_slice_in_dim(qv_sums, tensor_index * head_width, head_width, 1)
    in_share = lax.dynamic_slice_in_dim(in_sums, tensor_index * ffn_width, ffn_width, 0)
    back_out, back_grad = (
        lax.all_to_all(
            result.astype(jnp.bfloat16)[None, None], "dp", split_axis=2, concat_axis=0, tiled=True
        ),
        lax.all_to_all(
            input_grad.astype(jnp.bfloat16)[None, None],
            "dp",
            split_axis=2,
            concat_axis=0,
            tiled=True,
        ),
    )
    return (
        jnp.take(back_out, dealing, axis=0),
        jnp.take(back_grad, dealing, axis=0),
        qkv_sum,
        out_sum,
        in_sum,
        ffo_sum,
        qv_share,
        norm_sums[0],
        in_share,
        norm_sums[1],
        norm_sums[2],
        norm_sums[3],
        norm_sums[4],
        norm_sums[5],
    )


def solution(mesh):
    return jax.shard_map(
        per_device,
        mesh=mesh,
        in_specs=(
            P(None, "tensor", "dp", None),
            P(None, "tensor", "dp", None),
            P(),
            P(),
            P("dp", None, "tensor"),
            P("dp", "tensor"),
            P("dp", "tensor"),
            P("dp", "tensor"),
            P(None, "tensor"),
            P(),
            P("tensor"),
            P(),
            P(),
            P(),
            P(),
            P(),
        ),
        out_specs=(
            P(None, "tensor", "dp", None),
            P(None, "tensor", "dp", None),
            P("dp", None, "tensor"),
            P("dp", "tensor"),
            P("dp", "tensor"),
            P("dp", "tensor"),
            P(None, "tensor"),
            P(),
            P("tensor"),
            P(),
            P(),
            P(),
            P(),
            P(),
        ),
        check_vma=False,
    )
```

profile of v0, /device:TPU:0, one launch (start us, length us, event | category | flops | bytes accessed | tf_op | source)
XLA Modules:
  0.0 1286.9 jit_solution(3330152919851395239)
XLA Ops:
  16.4 53.0 %all_to_all.42 = bf16[16,1,64,768]{3,2,1,0:T(8,128)(2,1)} all-to-all(bf16[16,1,64,768]{3,2,1,0:T(8,128)(2,1)S(1)} %get-tuple-element.272), channel_id=1, replica_groups=mesh['dp'=16,'tensor'=2] {'dp'}, dimensions={0} | all-to-all | bytes 3145728 | tf_op jit(solution)/shard_map/all_to_all | solution.py:112
  70.2 23.6 %all_gather.30 = bf16[768,384]{1,0:T(8,128)(2,1)} all-gather(bf16[48,384]{1,0:T(8,128)(2,1)S(1)} %convert_element_type.160), channel_id=1, replica_groups=mesh['dp'=16,'tensor'=2] {'dp'}, dimensions={0}, use_global_device_ids=true | all-gather | bytes 626688 | tf_op jit(solution)/shard_map/all_gather | solution.py:134
  93.8 20.8 %all-gather.8.cloned.1.call-done = bf16[2048,768]{1,0:T(8,128)(2,1)} async-done(((bf16[1024,768]{1,0:T(8,128)(2,1)}), bf16[2048,768]{1,0:T(8,128)(2,1)}) %all-gather.8.cloned.1.call-update) | async-done | bytes 3145744 | tf_op jit(solution)/shard_map/all_gather | solution.py:145
  114.7 6.5 convolution_bitcast_fusion
  122.5 3.0 fusion.154
  125.6 3.1 copy.69
  128.6 5.8 copy.68
  134.4 5.7 copy.70
  140.1 5.2 fusion.129
  148.9 117.0 %while.28 = (s32[]{:T(128)}, bf16[6,2048,64]{1,2,0:T(8,128)(2,1)}, f32[6,2048]{1,0:T(8,128)}, bf16[6,2048,64]{2,1,0:T(8,128)(2,1)}, bf16[6,2048,64]{2,1,0:T(8,12...) while((s32[]{:T(128)}, bf16[6,2048,64]{1,2,0:T(8,128)(2,1)}, ...), condition=%wide.region_10.12_spmd.clone, body=%wide.region_1.11_spmd.clone.sunk | while | flops 1125128192 | bytes 70637272 | solution.py:152
  155.0 3.5 fusion.240
  159.8 2.9 fusion.241
  174.4 3.5 fusion.240
  179.2 2.9 fusion.241
  193.8 3.5 fusion.240
  198.6 2.9 fusion.241
  213.2 3.5 fusion.240
  218.0 2.9 fusion.241
  232.6 3.5 fusion.240
  237.4 2.9 fusion.241
  252.0 3.5 fusion.240
  256.8 2.9 fusion.241
  265.9 6.2 convolution_convert_fusion
  273.8 41.9 %reduce-scatter.9.cloned.1.call-done = bf16[1024,768]{1,0:T(8,128)(2,1)} async-done(((bf16[2048,768]{1,0:T(8,128)(2,1)}), bf16[1024,768]{1,0:T(8,128)(2,1)}) %reduce-scatter.9.cloned.1.call-update) | async-done | bytes 1572880 | tf_op jit(solution)/shard_map/reduce_scatter | solution.py:159
  321.6 39.1 %all-gather.14.cloned.1.call-done = bf16[768,1536]{1,0:T(8,128)(2,1)} async-done(((bf16[48,1536]{1,0:T(8,128)(2,1)}), bf16[768,1536]{1,0:T(8,128)(2,1)}) %all-gather.14.cloned.1.call-update) | async-done | bytes 2359312 | tf_op jit(solution)/shard_map/all_gather | solution.py:135
  360.7 45.1 %all-gather.12.cloned.1.call-done = bf16[2048,768]{1,0:T(8,128)(2,1)} async-done(((bf16[1024,768]{1,0:T(8,128)(2,1)}), bf16[2048,768]{1,0:T(8,128)(2,1)}) %all-gather.12.cloned.1.call-update) | async-done | bytes 3145744 | tf_op jit(solution)/shard_map/all_gather | solution.py:170
  405.8 34.6 %fusion.115 = (bf16[2048,1536]{1,0:T(8,128)(2,1)}, f32[2048,1536]{1,0:T(8,128)}) fusion(f32[1536]{0:T(1024)S(1)} %copy-done.49, bf16[2048,768]{1,0:T(8,128)(2,1)} %all-gather.12.cloned.1.call-done, bf16[768,1536]{1,0:T(8,128)(2,1)} %all-gather.14.cloned.1.call-done), kind=kOutput, calls=%fused_computation.175 | convolution fusion | flops 5039456256 | bytes 24385536 | tf_op jit(solution)/shard_map/dot_general | solution.py:171
  440.4 10.5 all-gather.16.cloned.1.call-done
  450.8 9.0 convolution_convert_fusion.2
  460.0 40.0 %all_to_all.43 = bf16[16,1,64,768]{3,2,1,0:T(8,128)(2,1)S(1)} all-to-all(bf16[16,1,64,768]{3,2,1,0:T(8,128)(2,1)} %get-tuple-element.271), channel_id=1, replica_groups=mesh['dp'=16,'tensor'=2] {'dp'}, dimensions={0} | all-to-all | bytes 3145728 | tf_op jit(solution)/shard_map/all_to_all | solution.py:115
  502.5 2.9 fusion.153
  508.6 3.4 fusion.151
  512.0 45.3 %all-gather.18.cloned.1.call-done = bf16[2048,768]{1,0:T(8,128)(2,1)} async-done(((bf16[1024,768]{1,0:T(8,128)(2,1)}), bf16[2048,768]{1,0:T(8,128)(2,1)}) %all-gather.18.cloned.1.call-update) | async-done | bytes 3145744 | tf_op jit(solution)/shard_map/all_gather | solution.py:194
  557.3 12.4 convert_reduce_fusion
  572.3 6.4 convolution_convert_fusion.1
  578.8 43.5 %reduce-scatter.13.cloned.1.call-done = bf16[1024,768]{1,0:T(8,128)(2,1)} async-done(((bf16[2048,768]{1,0:T(8,128)(2,1)}), bf16[1024,768]{1,0:T(8,128)(2,1)}) %reduce-scatter.13.cloned.1.call-update) | async-done | bytes 1572880 | tf_op jit(solution)/shard_map/reduce_scatter | solution.py:201
  622.4 4.6 multiply_reduce_fusion.4
  632.4 45.0 %all-gather.20.cloned.1.call-done = bf16[2048,768]{1,0:T(8,128)(2,1)} async-done(((bf16[1024,768]{1,0:T(8,128)(2,1)}), bf16[2048,768]{1,0:T(8,128)(2,1)}) %all-gather.20.cloned.1.call-update) | async-done | bytes 3145744 | tf_op jit(solution)/shard_map/all_gather | solution.py:213
  677.4 3.3 convolution_convert_fusion.3
  680.8 2.9 copy.72
  687.6 217.3 %while.29 = (s32[]{:T(128)}, bf16[6,2048,64]{1,2,0:T(8,128)(2,1)}, bf16[6,2048,64]{1,2,0:T(8,128)(2,1)}, bf16[6,2048,64]{1,2,0:T(8,128)(2,1)}, bf16[6,2048,64]{2...) while((s32[]{:T(128)}, bf16[6,2048,64]{1,2,0:T(8,128)(2,1)}, ...), condition=%wide.region_27.29_spmd.clone, body=%wide.region_22.28_spmd.clone.sunk | while | flops 2724331520 | bytes 161284432 | solution.py:218
  910.9 8.5 bitcast_convert_fusion
  921.3 9.6 fusion.157
  932.8 9.5 fusion.156
  943.7 4.8 fusion.155
  948.5 3.8 copy.87
  952.8 11.5 reduce.24
  964.3 4.7 reshape.275
  969.0 5.7 all-to-all-start.1
  974.7 8.7 fusion.138
  989.8 11.5 reduce.23
  1001.3 4.6 reshape.277
  1005.9 9.2 all-to-all-done.1
  1015.1 19.2 %all-to-all-start.3 = ((bf16[16,2,24576]{2,1,0:T(2,128)(2,1)}), bf16[16,2,24576]{2,1,0:T(2,128)(2,1)}, u32[]{:S(2)}, u32[]{:S(2)}) async-start(bf16[16,2,24576]{2,1,0:T(2,128)(2,1)} %reshape.277), calls=%async_computation.7 | async-start | bytes 3145728 | tf_op jit(solution)/shard_map/all_to_all | solution.py:277
  1034.4 10.1 reshape.276
  1044.5 3.4 copy.82
  1047.9 3.3 gather_fusion.1
  1052.3 48.6 %all-reduce = (f32[2,768]{1,0:T(2,128)S(1)}, f32[6,768]{1,0:T(8,128)S(1)}, f32[3072]{0:T(1024)S(1)}) all-reduce(f32[2,768]{1,0:T(2,128)S(1)} %maximum_dynamic-update-slice_fusion, f32[6,768]{1,0:T(8,128)S(1)} %stack.44, f32[3072]{0:T(1024)S(1)} %dynamic_update_slice.24), channel_id=1, replica_groups=mesh['dp'=16,'tensor'=2] {'dp','tensor'}, use_global_device_ids=true, to_apply=%region_35.37 | all-reduce | flops 9216 | bytes 73728 | tf_op jit(solution)/shard_map/psum | solution.py:270
  1102.8 8.1 reshape.278
  1112.3 3.3 gather_fusion.3
  1115.7 3.5 fusion.145
  1119.2 28.1 %reduce-scatter.21.cloned.1.call-done = f32[48,1536]{1,0:T(8,128)} async-done(((f32[768,1536]{1,0:T(8,128)}), f32[48,1536]{1,0:T(8,128)}) %reduce-scatter.21.cloned.1.call-update) | async-done | bytes 294928 | tf_op jit(solution)/shard_map/reduce_scatter | solution.py:255
  1147.3 61.5 %reduce-scatter.19.cloned.1.call-done = f32[48,384]{1,0:T(8,128)} async-done(((f32[768,384]{1,0:T(8,128)}), f32[48,384]{1,0:T(8,128)}) %reduce-scatter.19.cloned.1.call-update) | async-done | bytes 73744 | tf_op jit(solution)/shard_map/reduce_scatter | solution.py:254
  1208.7 71.4 %reduce-scatter.17.cloned.1.call-done = f32[48,3,384]{2,0,1:T(8,128)} async-done(((f32[768,3,384]{2,0,1:T(8,128)}), f32[48,3,384]{2,0,1:T(8,128)}) %reduce-scatter.17.cloned.1.call-update) | async-done | bytes 221200 | tf_op jit(solution)/shard_map/reduce_scatter | solution.py:253
  (484 shorter events, 356.2 us)
Async XLA Ops:
  7.2 5.0 copy-start
  7.2 86.6 %all-gather.10.cloned.1.call-start = ((), (), s32[]{:S(2)}) async-start(), calls=%async_computation.13 | async-start | bytes 1880064 | tf_op jit(solution)/shard_map/all_gather | solution.py:133
  9.0 105.7 %all-gather.8.cloned.1.call-start = ((), (), s32[]{:S(2)}) async-start(), calls=%async_computation.12 | async-start | bytes 4718592 | tf_op jit(solution)/shard_map/all_gather | solution.py:145
  16.4 53.1 %copy-start.43 = (f32[2,384]{1,0:T(2,128)S(1)}, f32[2,384]{1,0:T(2,128)}, u32[]{:S(2)}) copy-start(f32[2,384]{1,0:T(2,128)} %param.30) | copy-start | bytes 9220
  16.4 53.3 %copy-start.30 = (f32[48,384]{1,0:T(8,128)S(1)}, f32[48,384]{1,0:T(8,128)}, u32[]{:S(2)}) copy-start(f32[48,384]{1,0:T(8,128)} %param.27) | copy-start | bytes 221188
  16.4 53.3 %copy-start.50 = (s32[16]{0:T(128)S(1)}, s32[16]{0:T(128)}, u32[]{:S(2)}) copy-start(s32[16]{0:T(128)} %param.24) | copy-start | bytes 196
  69.4 246.3 %reduce-scatter.9.cloned.1.call-start = ((), (), s32[]{:S(2)}) async-start(), calls=%async_computation.14 | async-start | bytes 4718592 | tf_op jit(solution)/shard_map/reduce_scatter | solution.py:159
  140.1 5.2 copy-start.11
  155.0 3.5 copy-start.5
  174.4 3.5 copy-start.5
  193.8 3.5 copy-start.5
  213.2 3.5 copy-start.5
  232.6 3.5 copy-start.5
  252.0 3.5 copy-start.5
  265.9 6.2 copy-start.2
  272.0 43.6 %copy-start.29 = (f32[768]{0:T(1024)S(1)}, f32[768]{0:T(1024)}, u32[]{:S(2)}) copy-start(f32[768]{0:T(1024)} %param.31) | copy-start | bytes 9220
  272.0 43.6 %copy-start.4 = (bf16[16,1,64,768]{3,2,1,0:T(8,128)(2,1)S(1)}, bf16[16,1,64,768]{3,2,1,0:T(8,128)(2,1)}, u32[]{:S(2)}) copy-start(bf16[16,1,64,768]{3,2,1,0:T(8,128)(2,1)} %all_to_all.42) | copy-start | bytes 4718596
  272.1 88.6 %all-gather.14.cloned.1.call-start = ((), (), s32[]{:S(2)}) async-start(), calls=%async_computation.16 | async-start | bytes 2506752 | tf_op jit(solution)/shard_map/all_gather | solution.py:135
  273.7 45.0 %copy-start.31 = (f32[768]{0:T(1024)S(1)}, f32[768]{0:T(1024)}, u32[]{:S(2)}) copy-start(f32[768]{0:T(1024)} %param.34) | copy-start | bytes 9220
  273.7 45.0 %copy-start.38 = (f32[768]{0:T(1024)S(1)}, f32[768]{0:T(1024)}, u32[]{:S(2)}) copy-start(f32[768]{0:T(1024)} %param.35) | copy-start | bytes 9220
  273.7 132.0 %all-gather.12.cloned.1.call-start = ((), (), s32[]{:S(2)}) async-start(), calls=%async_computation.15 | async-start | bytes 4718592 | tf_op jit(solution)/shard_map/all_gather | solution.py:170
  318.7 87.1 %copy-start.49 = (f32[1536]{0:T(1024)S(1)}, f32[1536]{0:T(1024)}, u32[]{:S(2)}) copy-start(f32[1536]{0:T(1024)} %param.32) | copy-start | bytes 18436
  320.8 130.0 %all-gather.16.cloned.1.call-start = ((), (), s32[]{:S(2)}) async-start(), calls=%async_computation.17 | async-start | bytes 2506752 | tf_op jit(solution)/shard_map/all_gather | solution.py:136
  321.6 180.9 %reduce-scatter.11.cloned.1.call-start = ((), (), s32[]{:S(2)}) async-start(), calls=%async_computation.18 | async-start | bytes 4718592 | tf_op jit(solution)/shard_map/reduce_scatter | solution.py:173
  459.9 41.2 %copy-start.32 = (f32[768]{0:T(1024)S(1)}, f32[768]{0:T(1024)}, u32[]{:S(2)}) copy-start(f32[768]{0:T(1024)} %param.36) | copy-start | bytes 9220
  459.9 42.6 %copy-start.41 = (f32[768]{0:T(1024)S(1)}, f32[768]{0:T(1024)}, u32[]{:S(2)}) copy-start(f32[768]{0:T(1024)} %param.33) | copy-start | bytes 9220
  459.9 97.4 %all-gather.18.cloned.1.call-start = ((), (), s32[]{:S(2)}) async-start(), calls=%async_computation.19 | async-start | bytes 4718592 | tf_op jit(solution)/shard_map/all_gather | solution.py:194
  512.0 110.4 %reduce-scatter.13.cloned.1.call-start = ((), (), s32[]{:S(2)}) async-start(), calls=%async_computation.20 | async-start | bytes 4718592 | tf_op jit(solution)/shard_map/reduce_scatter | solution.py:201
  557.3 15.1 %copy-start.48 = (bf16[768,1536]{1,0:T(8,128)(2,1)S(1)}, bf16[768,1536]{1,0:T(8,128)(2,1)}, u32[]{:S(2)}) copy-start(bf16[768,1536]{1,0:T(8,128)(2,1)} %all-gather.14.cloned.1.call-done) | copy-start | bytes 7077892
  578.8 98.7 %all-gather.20.cloned.1.call-start = ((), (), s32[]{:S(2)}) async-start(), calls=%async_computation.21 | async-start | bytes 4718592 | tf_op jit(solution)/shard_map/all_gather | solution.py:213
  622.4 4.6 copy-start.10
  622.4 4.6 copy-start.21
  631.1 46.4 %copy-start.26 = (bf16[768,384]{1,0:T(8,128)(2,1)S(1)}, bf16[768,384]{1,0:T(8,128)(2,1)}, u32[]{:S(2)}) copy-start(bf16[768,384]{1,0:T(8,128)(2,1)} %all_gather.30) | copy-start | bytes 1769476
  632.4 351.1 %reduce-scatter.15.cloned.1.call-start = ((), (), s32[]{:S(2)}) async-start(), calls=%async_computation.22 | async-start | bytes 4718592 | tf_op jit(solution)/shard_map/reduce_scatter | solution.py:244
  683.6 4.0 copy-start.3
  687.8 3.6 copy-start.6
  724.0 3.6 copy-start.6
  760.1 3.6 copy-start.6
  796.2 3.6 copy-start.6
  832.4 3.6 copy-start.6
  868.5 3.6 copy-start.6
  904.9 2.8 copy-start.16
  904.9 4.4 copy-start.14
  919.5 199.7 %reduce-scatter.23.cloned.1.call-start = ((), (), s32[]{:S(2)}) async-start(), calls=%async_computation.26 | async-start | bytes 5013504 | tf_op jit(solution)/shard_map/reduce_scatter | solution.py:256
  930.9 216.3 %reduce-scatter.21.cloned.1.call-start = ((), (), s32[]{:S(2)}) async-start(), calls=%async_computation.25 | async-start | bytes 5013504 | tf_op jit(solution)/shard_map/reduce_scatter | solution.py:255
  942.3 266.4 %reduce-scatter.19.cloned.1.call-start = ((), (), s32[]{:S(2)}) async-start(), calls=%async_computation.24 | async-start | bytes 1253376 | tf_op jit(solution)/shard_map/reduce_scatter | solution.py:254
  964.3 10.4 copy-start.23
  964.3 10.4 copy-start.24
  969.0 46.1 %all-to-all-start.1 = ((bf16[16,2,24576]{2,1,0:T(2,128)(2,1)}), bf16[16,2,24576]{2,1,0:T(2,128)(2,1)}, u32[]{:S(2)}, u32[]{:S(2)}) async-start(bf16[16,2,24576]{2,1,0:T(2,128)(2,1)} %reshape.275), calls=%async_computation.3 | async-start | bytes 3145728 | tf_op jit(solution)/shard_map/all_to_all | solution.py:274
  974.7 305.5 %reduce-scatter.17.cloned.1.call-start = ((), (), s32[]{:S(2)}) async-start(), calls=%async_computation.23 | async-start | bytes 3760128 | tf_op jit(solution)/shard_map/reduce_scatter | solution.py:253
  1001.3 33.0 %copy-start.45 = (s32[16]{0:T(128)S(1)}, s32[16]{0:T(128)}, u32[]{:S(2)}) copy-start(s32[16]{0:T(128)} %get-tuple-element.277) | copy-start | bytes 196
  1001.3 33.0 %copy-start.36 = (f32[768]{0:T(1024)S(1)}, f32[768]{0:T(1024)}, u32[]{:S(2)}) copy-start(f32[768]{0:T(1024)} %get-tuple-element.194) | copy-start | bytes 9220
  1001.3 33.1 %copy-start.39 = (f32[768]{0:T(1024)S(1)}, f32[768]{0:T(1024)}, u32[]{:S(2)}) copy-start(f32[768]{0:T(1024)} %get-tuple-element.189) | copy-start | bytes 9220
  1015.1 87.7 %all-to-all-start.3 = ((bf16[16,2,24576]{2,1,0:T(2,128)(2,1)}), bf16[16,2,24576]{2,1,0:T(2,128)(2,1)}, u32[]{:S(2)}, u32[]{:S(2)}) async-start(bf16[16,2,24576]{2,1,0:T(2,128)(2,1)} %reshape.277), calls=%async_computation.7 | async-start | bytes 3145728 | tf_op jit(solution)/shard_map/all_to_all | solution.py:277
  1044.5 6.8 copy-start.40
  1044.5 7.1 copy-start.35
  1044.5 7.1 copy-start.34
  1044.5 7.1 copy-start.33
  1044.5 7.1 copy-start.37
  1044.5 7.2 copy-start.17
  1047.9 4.0 copy-start.15
  1110.9 4.7 copy-start.44
  1112.3 3.3 copy-start.20
  1115.7 164.5 %copy-start.1 = (bf16[16,1,64,768]{3,2,1,0:T(8,128)(2,1)S(1)}, bf16[16,1,64,768]{3,2,1,0:T(8,128)(2,1)}, u32[]{:S(2)}) copy-start(bf16[16,1,64,768]{3,2,1,0:T(8,128)(2,1)} %param.23) | copy-start | bytes 4718596
  (25 other events, 44.9 us)
Sparse Core Ops, SparseCore 0:
  10.9 53.5 all-gather.9
  69.5 45.1 all-gather.7
  272.2 43.4 reduce-scatter.8
  318.4 42.2 all-gather.13
  362.1 43.6 all-gather.11
  408.5 42.2 all-gather.15
  460.0 42.1 reduce-scatter.10
  512.1 45.1 all-gather.17
  578.9 43.4 reduce-scatter.12
  632.5 44.8 all-gather.19
  919.6 43.4 reduce-scatter.14
  967.3 94.5 reduce-scatter.22
  1066.4 80.8 reduce-scatter.20
  1151.3 57.3 reduce-scatter.18
  1213.0 67.1 reduce-scatter.16
where the time goes:
time: 1300 us; the launch traced here: 1290 us
  waiting for transfers between devices  462 us (36%)
  matrix products  388 us (30%)
  blocking collectives  165 us (13%)
  local copies, waits for them, and re-layouts  116 us (9%)
  other arithmetic  113 us (9%)
  starting transfers between devices  25.9 us (2%)
  between operations  14.7 us (1%)
    dot_general x75, matrix products, contract_last(): lax.dot_general(left_side, right_side, (((1,), (1,)), ((), ())), preferre...  168 us
    dot_general x51, matrix products, contract_first(): lax.dot_general(left_side, right_side, (((0,), (0,)), ((), ())), preferre...  97.7 us
    reduce_scatter x1, waiting for transfers between devices, per_device(): lax.psum_scatter(qkv_weight_grad, 'dp', scatter_dimension=0, tiled=True)  71.4 us
    reduce_scatter x1, waiting for transfers between devices, per_device(): lax.psum_scatter(out_weight_grad, 'dp', scatter_dimension=0, tiled=True)  61.5 us
    all_to_all x1, blocking collectives, per_device(): lax.all_to_all(jnp.take(x_in, owners, axis=0), 'dp', split_axis=0, concat...  53 us
    psum x1, blocking collectives, per_device(): lax.psum((norm_terms, qv_padded, in_padded), ('dp', 'tensor'))  48.6 us
    unnamed x103, local copies, waits for them, and re-layouts  46.6 us
    all_gather x1, waiting for transfers between devices, per_device(): lax.all_gather(final_grad.astype(jnp.bfloat16), 'tensor', axis=0, tiled=T...  45.3 us
  transfers between devices with their start and end apart: 17, of which 12 were waited for; matrix products, arithmetic and copies ran while one was open for 12% of the time, Pallas kernels for 0%

commit v1 on v0

--- a/solution.py
+++ b/solution.py
@@ -1,9 +1,26 @@
+import functools
 import jax
 import jax.numpy as jnp
 from jax import lax
 from jax.sharding import PartitionSpec as P
 
 HEAD_DIM = 64
+
+
+def unit_remake(shard_in, k_dim):
+    front = jax.lax.axis_size("tensor")
+    tile_out, m_next, item_now = (front, jax.lax.axis_index("tensor"), shard_in.shape[k_dim])
+    carry, left_arr = (shard_in, 1)
+    while left_arr < tile_out:
+        outer = jax.lax.ppermute(
+            carry, "tensor", [(no, (no - left_arr) % tile_out) for no in range(tile_out)]
+        )
+        carry = jnp.concatenate([carry, outer], k_dim)
+        left_arr = 2 * left_arr
+    return jnp.roll(carry, m_next * item_now, k_dim)
+
+
+_guide_frames = functools.partial(unit_remake, k_dim=0)
 
 
 def slot_owner(dealing):
@@ -167,7 +184,7 @@
     first_norm, normed_one, inverse_one = norm_forward(
         tokens_half.astype(jnp.float32) + attn_half + b_out, ln1_gain, ln1_bias
     )
-    first_full = lax.all_gather(first_norm.astype(jnp.bfloat16), "tensor", axis=0, tiled=True)
+    first_full = _guide_frames(first_norm.astype(jnp.bfloat16))
     hidden = jnp.dot(first_full, in_weight, preferred_element_type=jnp.float32) + b_in
     active = jax.nn.gelu(hidden, approximate=False).astype(jnp.bfloat16)
     ffn_half = lax.psum_scatter(

time: 1300 us -> 1250 us (0.962)
  waiting for transfers between devices: 462 us -> 408 us
    all_gather x1 -> x0, waiting for transfers between devices: 45.1 us -> none  [per_device(): lax.all_gather(first_norm.astype(jnp.bfloat16), 'tensor', axis=0, tiled=T...]
    all_gather x1, waiting for transfers between devices: 39.1 us -> 0.01 us  [per_device(): lax.all_gather(w_in.astype(jnp.bfloat16), 'dp', axis=0, tiled=True)]
    ppermute x0 -> x1, waiting for transfers between devices: none -> 35.1 us  [unit_remake(): jax.lax.ppermute(carry, 'tensor', [(no, (no - left_arr) % tile_out) for n...]
  transfers between devices with their start and end apart: 17 -> 17, of which waited for: 12 -> 11; matrix products, arithmetic and copies ran while one was open for 12% -> 13% of each run, Pallas kernels for 0% -> 0%
where the time goes in v1:
time: 1250 us; the launch traced here: 1240 us
  waiting for transfers between devices  408 us (33%)
  matrix products  388 us (31%)
  blocking collectives  165 us (13%)
  other arithmetic  119 us (10%)
  local copies, waits for them, and re-layouts  116 us (9%)
  starting transfers between devices  26.2 us (2%)
  between operations  14.7 us (1%)
    dot_general x75, matrix products, contract_last(): lax.dot_general(left_side, right_side, (((1,), (1,)), ((), ())), preferre...  168 us
    dot_general x51, matrix products, contract_first(): lax.dot_general(left_side, right_side, (((0,), (0,)), ((), ())), preferre...  97.7 us
    reduce_scatter x1, waiting for transfers between devices, per_device(): lax.psum_scatter(qkv_weight_grad, 'dp', scatter_dimension=0, tiled=True)  71.6 us
    reduce_scatter x1, waiting for transfers between devices, per_device(): lax.psum_scatter(out_weight_grad, 'dp', scatter_dimension=0, tiled=True)  61.6 us
    all_to_all x1, blocking collectives, per_device(): lax.all_to_all(jnp.take(x_in, owners, axis=0), 'dp', split_axis=0, concat...  53 us
    psum x1, blocking collectives, per_device(): lax.psum((norm_terms, qv_padded, in_padded), ('dp', 'tensor'))  48.7 us
    unnamed x103, local copies, waits for them, and re-layouts  46.6 us
    all_gather x1, waiting for transfers between devices, per_device(): lax.all_gather(final_grad.astype(jnp.bfloat16), 'tensor', axis=0, tiled=T...  45.3 us
  transfers between devices with their start and end apart: 17, of which 11 were waited for; matrix products, arithmetic and copies ran while one was open for 13% of the time, Pallas kernels for 0%

profile of v1, /device:TPU:0, one launch (start us, length us, event | category | flops | bytes accessed | tf_op | source)
XLA Modules:
  0.0 1240.5 jit_solution(11277169149185792513)
XLA Ops:
  16.4 53.0 %all_to_all.42 = bf16[16,1,64,768]{3,2,1,0:T(8,128)(2,1)} all-to-all(bf16[16,1,64,768]{3,2,1,0:T(8,128)(2,1)S(1)} %get-tuple-element.272), channel_id=1, replica_groups=mesh['dp'=16,'tensor'=2] {'dp'}, dimensions={0} | all-to-all | bytes 3145728 | tf_op jit(solution)/shard_map/all_to_all | solution.py:129
  70.2 23.6 %all_gather.27 = bf16[768,384]{1,0:T(8,128)(2,1)} all-gather(bf16[48,384]{1,0:T(8,128)(2,1)S(1)} %convert_element_type.160), channel_id=1, replica_groups=mesh['dp'=16,'tensor'=2] {'dp'}, dimensions={0}, use_global_device_ids=true | all-gather | bytes 626688 | tf_op jit(solution)/shard_map/all_gather | solution.py:151
  93.8 20.8 %all-gather.7.cloned.1.call-done = bf16[2048,768]{1,0:T(8,128)(2,1)} async-done(((bf16[1024,768]{1,0:T(8,128)(2,1)}), bf16[2048,768]{1,0:T(8,128)(2,1)}) %all-gather.7.cloned.1.call-update) | async-done | bytes 3145744 | tf_op jit(solution)/shard_map/all_gather | solution.py:162
  114.7 6.5 convolution_bitcast_fusion
  122.5 3.0 fusion.157
  125.6 3.1 copy.69
  128.6 5.8 copy.68
  134.4 5.7 copy.70
  140.1 5.2 fusion.129
  148.9 117.0 %while.28 = (s32[]{:T(128)}, bf16[6,2048,64]{1,2,0:T(8,128)(2,1)}, f32[6,2048]{1,0:T(8,128)}, bf16[6,2048,64]{2,1,0:T(8,128)(2,1)}, bf16[6,2048,64]{2,1,0:T(8,12...) while((s32[]{:T(128)}, bf16[6,2048,64]{1,2,0:T(8,128)(2,1)}, ...), condition=%wide.region_10.12_spmd.clone, body=%wide.region_1.11_spmd.clone.sunk | while | flops 1125128192 | bytes 70637272 | solution.py:169
  155.0 3.5 fusion.243
  159.8 2.9 fusion.244
  174.4 3.5 fusion.243
  179.2 2.9 fusion.244
  193.8 3.5 fusion.243
  198.6 2.9 fusion.244
  213.2 3.5 fusion.243
  218.0 2.9 fusion.244
  232.6 3.5 fusion.243
  237.4 2.9 fusion.244
  252.0 3.5 fusion.243
  256.8 2.9 fusion.244
  265.9 6.2 convolution_convert_fusion
  273.8 41.9 %reduce-scatter.9.cloned.1.call-done = bf16[1024,768]{1,0:T(8,128)(2,1)} async-done(((bf16[2048,768]{1,0:T(8,128)(2,1)}), bf16[1024,768]{1,0:T(8,128)(2,1)}) %reduce-scatter.9.cloned.1.call-update) | async-done | bytes 1572880 | tf_op jit(solution)/shard_map/reduce_scatter | solution.py:176
  321.9 35.1 %collective-permute-done = bf16[1024,768]{1,0:T(8,128)(2,1)} collective-permute-done((bf16[1024,768]{1,0:T(8,128)(2,1)}, bf16[1024,768]{1,0:T(8,128)(2,1)}, u32[]{:S(2)}, u32[]{:S(2)}) %collective-permute-start) | collective-permute-done | bytes 1572896 | tf_op jit(solution)/shard_map/ppermute | solution.py:15
  357.0 6.6 fusion.133
  363.6 34.6 %fusion.115 = (bf16[2048,1536]{1,0:T(8,128)(2,1)}, f32[2048,1536]{1,0:T(8,128)}) fusion(f32[1536]{0:T(1024)S(1)} %copy-done.49, bf16[2048,768]{1,0:T(8,128)(2,1)} %fusion.133, bf16[768,1536]{1,0:T(8,128)(2,1)} %all-gather.11.cloned.1.call-done), kind=kOutput, calls=%fused_computation.175 | convolution fusion | flops 5039456256 | bytes 24385536 | tf_op jit(solution)/shard_map/dot_general | solution.py:188
  398.2 6.1 all-gather.13.cloned.1.call-done
  404.3 9.0 convolution_convert_fusion.2
  413.4 40.0 %all_to_all.43 = bf16[16,1,64,768]{3,2,1,0:T(8,128)(2,1)S(1)} all-to-all(bf16[16,1,64,768]{3,2,1,0:T(8,128)(2,1)} %get-tuple-element.271), channel_id=1, replica_groups=mesh['dp'=16,'tensor'=2] {'dp'}, dimensions={0} | all-to-all | bytes 3145728 | tf_op jit(solution)/shard_map/all_to_all | solution.py:132
  456.0 2.9 fusion.156
  462.1 3.4 fusion.154
  465.5 45.3 %all-gather.15.cloned.1.call-done = bf16[2048,768]{1,0:T(8,128)(2,1)} async-done(((bf16[1024,768]{1,0:T(8,128)(2,1)}), bf16[2048,768]{1,0:T(8,128)(2,1)}) %all-gather.15.cloned.1.call-update) | async-done | bytes 3145744 | tf_op jit(solution)/shard_map/all_gather | solution.py:211
  510.8 12.4 convert_reduce_fusion
  525.8 6.4 convolution_convert_fusion.1
  532.3 43.5 %reduce-scatter.13.cloned.1.call-done = bf16[1024,768]{1,0:T(8,128)(2,1)} async-done(((bf16[2048,768]{1,0:T(8,128)(2,1)}), bf16[1024,768]{1,0:T(8,128)(2,1)}) %reduce-scatter.13.cloned.1.call-update) | async-done | bytes 1572880 | tf_op jit(solution)/shard_map/reduce_scatter | solution.py:218
  575.9 4.6 multiply_reduce_fusion.4
  585.9 45.0 %all-gather.17.cloned.1.call-done = bf16[2048,768]{1,0:T(8,128)(2,1)} async-done(((bf16[1024,768]{1,0:T(8,128)(2,1)}), bf16[2048,768]{1,0:T(8,128)(2,1)}) %all-gather.17.cloned.1.call-update) | async-done | bytes 3145744 | tf_op jit(solution)/shard_map/all_gather | solution.py:230
  630.9 3.3 convolution_convert_fusion.3
  634.3 2.9 copy.72
  641.1 217.3 %while.29 = (s32[]{:T(128)}, bf16[6,2048,64]{1,2,0:T(8,128)(2,1)}, bf16[6,2048,64]{1,2,0:T(8,128)(2,1)}, bf16[6,2048,64]{1,2,0:T(8,128)(2,1)}, bf16[6,2048,64]{2...) while((s32[]{:T(128)}, bf16[6,2048,64]{1,2,0:T(8,128)(2,1)}, ...), condition=%wide.region_27.29_spmd.clone, body=%wide.region_22.28_spmd.clone.sunk | while | flops 2724331520 | bytes 161284432 | solution.py:235
  864.4 8.5 bitcast_convert_fusion
  874.8 9.6 fusion.160
  886.3 9.5 fusion.159
  897.2 4.8 fusion.158
  902.0 3.8 copy.87
  906.3 11.5 reduce.24
  917.8 4.7 reshape.275
  922.5 5.6 all-to-all-start.1
  928.2 8.7 fusion.141
  943.2 11.5 reduce.23
  954.8 4.6 reshape.277
  959.4 9.2 all-to-all-done.1
  968.6 19.2 %all-to-all-start.3 = ((bf16[16,2,24576]{2,1,0:T(2,128)(2,1)}), bf16[16,2,24576]{2,1,0:T(2,128)(2,1)}, u32[]{:S(2)}, u32[]{:S(2)}) async-start(bf16[16,2,24576]{2,1,0:T(2,128)(2,1)} %reshape.277), calls=%async_computation.7 | async-start | bytes 3145728 | tf_op jit(solution)/shard_map/all_to_all | solution.py:294
  987.9 10.1 reshape.276
  998.0 3.4 copy.82
  1001.4 3.3 gather_fusion.1
  1005.7 48.7 %all-reduce = (f32[2,768]{1,0:T(2,128)S(1)}, f32[6,768]{1,0:T(8,128)S(1)}, f32[3072]{0:T(1024)S(1)}) all-reduce(f32[2,768]{1,0:T(2,128)S(1)} %maximum_dynamic-update-slice_fusion, f32[6,768]{1,0:T(8,128)S(1)} %stack.44, f32[3072]{0:T(1024)S(1)} %dynamic_update_slice.24), channel_id=1, replica_groups=mesh['dp'=16,'tensor'=2] {'dp','tensor'}, use_global_device_ids=true, to_apply=%region_35.37 | all-reduce | flops 9216 | bytes 73728 | tf_op jit(solution)/shard_map/psum | solution.py:287
  1056.3 8.1 reshape.278
  1065.8 3.3 gather_fusion.3
  1069.1 3.5 fusion.148
  1072.7 27.9 %reduce-scatter.21.cloned.1.call-done = f32[48,1536]{1,0:T(8,128)} async-done(((f32[768,1536]{1,0:T(8,128)}), f32[48,1536]{1,0:T(8,128)}) %reduce-scatter.21.cloned.1.call-update) | async-done | bytes 294928 | tf_op jit(solution)/shard_map/reduce_scatter | solution.py:272
  1100.5 61.6 %reduce-scatter.19.cloned.1.call-done = f32[48,384]{1,0:T(8,128)} async-done(((f32[768,384]{1,0:T(8,128)}), f32[48,384]{1,0:T(8,128)}) %reduce-scatter.19.cloned.1.call-update) | async-done | bytes 73744 | tf_op jit(solution)/shard_map/reduce_scatter | solution.py:271
  1162.1 71.6 %reduce-scatter.17.cloned.1.call-done = f32[48,3,384]{2,0,1:T(8,128)} async-done(((f32[768,3,384]{2,0,1:T(8,128)}), f32[48,3,384]{2,0,1:T(8,128)}) %reduce-scatter.17.cloned.1.call-update) | async-done | bytes 221200 | tf_op jit(solution)/shard_map/reduce_scatter | solution.py:270
  (484 shorter events, 356.4 us)
Async XLA Ops:
  7.2 5.0 copy-start
  7.2 86.6 %all-gather.9.cloned.1.call-start = ((), (), s32[]{:S(2)}) async-start(), calls=%async_computation.13 | async-start | bytes 1880064 | tf_op jit(solution)/shard_map/all_gather | solution.py:150
  9.0 105.7 %all-gather.7.cloned.1.call-start = ((), (), s32[]{:S(2)}) async-start(), calls=%async_computation.12 | async-start | bytes 4718592 | tf_op jit(solution)/shard_map/all_gather | solution.py:162
  16.4 53.1 %copy-start.44 = (f32[2,384]{1,0:T(2,128)S(1)}, f32[2,384]{1,0:T(2,128)}, u32[]{:S(2)}) copy-start(f32[2,384]{1,0:T(2,128)} %param.30) | copy-start | bytes 9220
  16.4 53.3 %copy-start.31 = (f32[48,384]{1,0:T(8,128)S(1)}, f32[48,384]{1,0:T(8,128)}, u32[]{:S(2)}) copy-start(f32[48,384]{1,0:T(8,128)} %param.27) | copy-start | bytes 221188
  16.4 53.3 %copy-start.50 = (s32[16]{0:T(128)S(1)}, s32[16]{0:T(128)}, u32[]{:S(2)}) copy-start(s32[16]{0:T(128)} %param.24) | copy-start | bytes 196
  69.4 246.3 %reduce-scatter.9.cloned.1.call-start = ((), (), s32[]{:S(2)}) async-start(), calls=%async_computation.14 | async-start | bytes 4718592 | tf_op jit(solution)/shard_map/reduce_scatter | solution.py:176
  140.1 5.2 copy-start.11
  155.0 3.5 copy-start.5
  174.4 3.5 copy-start.5
  193.8 3.5 copy-start.5
  213.2 3.5 copy-start.5
  232.6 3.5 copy-start.5
  252.0 3.5 copy-start.5
  265.9 6.2 copy-start.2
  272.0 43.6 %copy-start.30 = (f32[768]{0:T(1024)S(1)}, f32[768]{0:T(1024)}, u32[]{:S(2)}) copy-start(f32[768]{0:T(1024)} %param.31) | copy-start | bytes 9220
  272.0 43.6 %copy-start.4 = (bf16[16,1,64,768]{3,2,1,0:T(8,128)(2,1)S(1)}, bf16[16,1,64,768]{3,2,1,0:T(8,128)(2,1)}, u32[]{:S(2)}) copy-start(bf16[16,1,64,768]{3,2,1,0:T(8,128)(2,1)} %all_to_all.42) | copy-start | bytes 4718596
  272.1 91.5 %all-gather.11.cloned.1.call-start = ((), (), s32[]{:S(2)}) async-start(), calls=%async_computation.15 | async-start | bytes 2506752 | tf_op jit(solution)/shard_map/all_gather | solution.py:152
  273.7 45.0 %copy-start.32 = (f32[768]{0:T(1024)S(1)}, f32[768]{0:T(1024)}, u32[]{:S(2)}) copy-start(f32[768]{0:T(1024)} %param.34) | copy-start | bytes 9220
  273.7 45.0 %copy-start.39 = (f32[768]{0:T(1024)S(1)}, f32[768]{0:T(1024)}, u32[]{:S(2)}) copy-start(f32[768]{0:T(1024)} %param.35) | copy-start | bytes 9220
  273.7 130.6 %all-gather.13.cloned.1.call-start = ((), (), s32[]{:S(2)}) async-start(), calls=%async_computation.16 | async-start | bytes 2506752 | tf_op jit(solution)/shard_map/all_gather | solution.py:153
  320.8 36.3 %collective-permute-start = (bf16[1024,768]{1,0:T(8,128)(2,1)}, bf16[1024,768]{1,0:T(8,128)(2,1)}, u32[]{:S(2)}, u32[]{:S(2)}) collective-permute-start(bf16[1024,768]{1,0:T(8,128)(2,1)} %fusion.144), channel_id=1, source_target_pairs={{0,1},{1,0},{2,3},{3,2},{4,5},{5,4},{6,7},{7,6},{8,9},{9,8},{10,11... | collective-permute-start | bytes 4718600 | tf_op jit(solution)/shard_map/ppermute | solution.py:15
  321.8 134.2 %reduce-scatter.11.cloned.1.call-start = ((), (), s32[]{:S(2)}) async-start(), calls=%async_computation.17 | async-start | bytes 4718592 | tf_op jit(solution)/shard_map/reduce_scatter | solution.py:190
  321.9 41.7 %copy-start.49 = (f32[1536]{0:T(1024)S(1)}, f32[1536]{0:T(1024)}, u32[]{:S(2)}) copy-start(f32[1536]{0:T(1024)} %param.32) | copy-start | bytes 18436
  413.3 41.2 %copy-start.33 = (f32[768]{0:T(1024)S(1)}, f32[768]{0:T(1024)}, u32[]{:S(2)}) copy-start(f32[768]{0:T(1024)} %param.36) | copy-start | bytes 9220
  413.4 42.6 %copy-start.42 = (f32[768]{0:T(1024)S(1)}, f32[768]{0:T(1024)}, u32[]{:S(2)}) copy-start(f32[768]{0:T(1024)} %param.33) | copy-start | bytes 9220
  413.4 97.4 %all-gather.15.cloned.1.call-start = ((), (), s32[]{:S(2)}) async-start(), calls=%async_computation.18 | async-start | bytes 4718592 | tf_op jit(solution)/shard_map/all_gather | solution.py:211
  465.5 110.4 %reduce-scatter.13.cloned.1.call-start = ((), (), s32[]{:S(2)}) async-start(), calls=%async_computation.19 | async-start | bytes 4718592 | tf_op jit(solution)/shard_map/reduce_scatter | solution.py:218
  510.8 15.1 %copy-start.48 = (bf16[768,1536]{1,0:T(8,128)(2,1)S(1)}, bf16[768,1536]{1,0:T(8,128)(2,1)}, u32[]{:S(2)}) copy-start(bf16[768,1536]{1,0:T(8,128)(2,1)} %all-gather.11.cloned.1.call-done) | copy-start | bytes 7077892
  532.3 98.6 %all-gather.17.cloned.1.call-start = ((), (), s32[]{:S(2)}) async-start(), calls=%async_computation.20 | async-start | bytes 4718592 | tf_op jit(solution)/shard_map/all_gather | solution.py:230
  575.9 4.6 copy-start.10
  575.9 4.6 copy-start.21
  584.5 46.4 %copy-start.27 = (bf16[768,384]{1,0:T(8,128)(2,1)S(1)}, bf16[768,384]{1,0:T(8,128)(2,1)}, u32[]{:S(2)}) copy-start(bf16[768,384]{1,0:T(8,128)(2,1)} %all_gather.27) | copy-start | bytes 1769476
  585.8 351.1 %reduce-scatter.15.cloned.1.call-start = ((), (), s32[]{:S(2)}) async-start(), calls=%async_computation.21 | async-start | bytes 4718592 | tf_op jit(solution)/shard_map/reduce_scatter | solution.py:261
  637.1 4.0 copy-start.3
  641.2 3.7 copy-start.6
  677.4 3.6 copy-start.6
  713.6 3.6 copy-start.6
  749.7 3.6 copy-start.6
  785.9 3.6 copy-start.6
  822.0 3.6 copy-start.6
  858.4 2.8 copy-start.16
  858.4 4.4 copy-start.14
  873.0 199.7 %reduce-scatter.23.cloned.1.call-start = ((), (), s32[]{:S(2)}) async-start(), calls=%async_computation.25 | async-start | bytes 5013504 | tf_op jit(solution)/shard_map/reduce_scatter | solution.py:273
  884.4 216.1 %reduce-scatter.21.cloned.1.call-start = ((), (), s32[]{:S(2)}) async-start(), calls=%async_computation.24 | async-start | bytes 5013504 | tf_op jit(solution)/shard_map/reduce_scatter | solution.py:272
  895.8 266.4 %reduce-scatter.19.cloned.1.call-start = ((), (), s32[]{:S(2)}) async-start(), calls=%async_computation.23 | async-start | bytes 1253376 | tf_op jit(solution)/shard_map/reduce_scatter | solution.py:271
  917.8 10.4 copy-start.24
  917.8 10.4 copy-start.25
  922.5 46.1 %all-to-all-start.1 = ((bf16[16,2,24576]{2,1,0:T(2,128)(2,1)}), bf16[16,2,24576]{2,1,0:T(2,128)(2,1)}, u32[]{:S(2)}, u32[]{:S(2)}) async-start(bf16[16,2,24576]{2,1,0:T(2,128)(2,1)} %reshape.275), calls=%async_computation.3 | async-start | bytes 3145728 | tf_op jit(solution)/shard_map/all_to_all | solution.py:291
  928.1 305.6 %reduce-scatter.17.cloned.1.call-start = ((), (), s32[]{:S(2)}) async-start(), calls=%async_computation.22 | async-start | bytes 3760128 | tf_op jit(solution)/shard_map/reduce_scatter | solution.py:270
  954.8 33.0 %copy-start.46 = (s32[16]{0:T(128)S(1)}, s32[16]{0:T(128)}, u32[]{:S(2)}) copy-start(s32[16]{0:T(128)} %get-tuple-element.277) | copy-start | bytes 196
  954.8 33.1 %copy-start.37 = (f32[768]{0:T(1024)S(1)}, f32[768]{0:T(1024)}, u32[]{:S(2)}) copy-start(f32[768]{0:T(1024)} %get-tuple-element.194) | copy-start | bytes 9220
  954.8 33.1 %copy-start.40 = (f32[768]{0:T(1024)S(1)}, f32[768]{0:T(1024)}, u32[]{:S(2)}) copy-start(f32[768]{0:T(1024)} %get-tuple-element.189) | copy-start | bytes 9220
  968.6 87.7 %all-to-all-start.3 = ((bf16[16,2,24576]{2,1,0:T(2,128)(2,1)}), bf16[16,2,24576]{2,1,0:T(2,128)(2,1)}, u32[]{:S(2)}, u32[]{:S(2)}) async-start(bf16[16,2,24576]{2,1,0:T(2,128)(2,1)} %reshape.277), calls=%async_computation.7 | async-start | bytes 3145728 | tf_op jit(solution)/shard_map/all_to_all | solution.py:294
  997.9 6.8 copy-start.41
  997.9 7.1 copy-start.36
  997.9 7.1 copy-start.35
  997.9 7.1 copy-start.34
  997.9 7.1 copy-start.38
  997.9 7.2 copy-start.17
  1001.4 4.0 copy-start.15
  1064.4 4.7 copy-start.45
  1065.8 3.3 copy-start.20
  1069.1 164.6 %copy-start.1 = (bf16[16,1,64,768]{3,2,1,0:T(8,128)(2,1)S(1)}, bf16[16,1,64,768]{3,2,1,0:T(8,128)(2,1)}, u32[]{:S(2)}) copy-start(bf16[16,1,64,768]{3,2,1,0:T(8,128)(2,1)} %param.23) | copy-start | bytes 4718596
  (25 other events, 45.2 us)
Sparse Core Ops, SparseCore 0:
  10.9 53.5 all-gather.8
  69.5 45.1 all-gather.6
  272.2 43.4 reduce-scatter.8
  318.4 42.1 all-gather.10
  363.2 41.0 all-gather.12
  413.5 42.1 reduce-scatter.10
  465.6 45.1 all-gather.14
  532.4 43.3 reduce-scatter.12
  586.0 44.9 all-gather.16
  873.1 43.3 reduce-scatter.14
  921.0 94.4 reduce-scatter.22
  1019.8 80.7 reduce-scatter.20
  1104.7 57.3 reduce-scatter.18
  1166.4 67.2 reduce-scatter.16
